TPU v7x, 256 devices: a whole 4x4x8 slice. The times are simulated.
256 devices in a mesh: expert: 64 (over z, y, core), dp: 4 (over x).
Axes of the slice: x: 4, y: 4, z: 8, core: 2. Of those that a mesh axis runs over, the one named last changes fastest.
Arguments:
- tokens: bfloat16 [16384, 2880], P(('expert', 'dp')), may hold values from -6 to 6
- expert_ids: int32 [16384, 4], P(('expert', 'dp')), may hold values from 0 to 63, all different within a row; in each aligned block of 64 rows (0 to 63, 64 to 127, ...) at most 6 rows name the same one
- gate_logits: float32 [16384, 4], P(('expert', 'dp')), may hold values from -3 to 3
- w_gate: bfloat16 [64, 2880, 1536], P('expert', None, 'dp'), may hold values from -0.109375 to 0.109375
- w_up: bfloat16 [64, 2880, 1536], P('expert', None, 'dp'), may hold values from -0.109375 to 0.109375
- w_down: bfloat16 [64, 1536, 2880], P('expert', 'dp'), may hold values from -0.15625 to 0.15625
Outputs:
- mixed: bfloat16 [16384, 2880], P(('expert', 'dp'))
Inputs may be any that keep to these rules, and one draw needn't show every extreme that they name: `expert_ids`: each row names 4 different experts. Among the 64 rows of one device no expert is named more than 6 times, and every expert is named somewhere.
All inputs are finite; a program needn't handle non-finite values.
Results may differ from a plain program's by a relative error of at most 0.012.
Values may be sent and summed in bfloat16 or wider, within the bound.
No kernel may reach another device: no remote copies, remote signals or barrier semaphores. Data moves between devices by JAX's collectives and lax.ppermute only.
A program may use at most 128 MiB of HBM per device.

v0:
```python
import jax
import jax.numpy as jnp
from jax import lax
from jax.sharding import PartitionSpec as P


def expert_rows(tile_in, gate_w, up_w, down_w):
    gate_val = jnp.dot(tile_in, gate_w, preferred_element_type=jnp.float32)
    up_val = jnp.dot(tile_in, up_w, preferred_element_type=jnp.float32)
    hidden = ((up_val + 1.0) * gate_val * jax.nn.sigmoid(1.702 * gate_val)).astype(jnp.bfloat16)
    return jnp.dot(hidden, down_w, preferred_element_type=jnp.float32).astype(jnp.bfloat16)


def run_tiles(packed, first_row, last_row, gate_w, up_w, down_w):
    tile_rows = 128
    n_tiles = jnp.maximum(last_row - first_row + tile_rows - 1, 0) // tile_rows
    result_buf = jnp.zeros((packed.shape[0], down_w.shape[1]), jnp.bfloat16)

    def advance(index_t, buffer):
        at_row = first_row + index_t * tile_rows
        tile_in = lax.dynamic_slice_in_dim(packed, at_row, tile_rows, 0)
        return lax.dynamic_update_slice_in_dim(
            buffer, expert_rows(tile_in, gate_w, up_w, down_w), at_row, 0
        )

    return lax.fori_loop(0, n_tiles, advance, result_buf)


def per_device(tokens, expert_ids, gate_logits, w_gate, w_up, w_down):
    n_rows, width = tokens.shape
    n_tops = expert_ids.shape[1]
    n_exp = lax.axis_size("expert")
    n_dp = lax.axis_size("dp")
    slot_cap = max(2, 3 * n_rows * n_tops // (2 * n_exp))
    tile_rows = 128
    flat_ids = expert_ids.reshape(-1)
    onehot = (flat_ids[:, None] == jnp.arange(n_exp, dtype=jnp.int32)[None, :]).astype(jnp.int32)
    rank_in = jnp.sum((jnp.cumsum(onehot, axis=0) - onehot) * onehot, axis=1)
    counts = jnp.sum(onehot, axis=0)
    slot_idx = flat_ids * slot_cap + rank_in
    source = (
        jnp.zeros((n_exp * slot_cap,), jnp.int32)
        .at[slot_idx]
        .set(jnp.arange(n_rows * n_tops, dtype=jnp.int32) // n_tops)
    )
    filled = (jnp.arange(slot_cap)[None, :] < counts[:, None]).reshape(-1)
    outgoing = jnp.where(filled[:, None], tokens[source], jnp.zeros_like(tokens[source])).reshape(
        n_exp, slot_cap, width
    )
    rows_mid, counts_mid = (
        lax.all_to_all(outgoing, "expert", split_axis=0, concat_axis=0, tiled=True),
        lax.all_to_all(counts[:, None], "expert", split_axis=0, concat_axis=0, tiled=True),
    )
    rows_in, counts_in = (
        lax.all_gather(rows_mid, "dp", axis=0, tiled=True),
        lax.all_gather(counts_mid, "dp", axis=0, tiled=True),
    )
    rows_flat = rows_in.reshape(-1, width)
    total_rows = rows_flat.shape[0]
    live_row = (jnp.arange(slot_cap)[None, :] < counts_in.reshape(-1)[:, None]).reshape(-1)
    position = jnp.cumsum(live_row.astype(jnp.int32)) - 1
    live_total = jnp.sum(live_row.astype(jnp.int32))
    padded = (total_rows + tile_rows - 1) // tile_rows * tile_rows + tile_rows
    gather_idx = (
        jnp.zeros((padded,), jnp.int32)
        .at[jnp.where(live_row, position, padded)]
        .set(jnp.arange(total_rows, dtype=jnp.int32), mode="drop")
    )
    packed = rows_flat[gather_idx]
    gate_w = w_gate[0]
    up_w = w_up[0]
    down_w = w_down[0]
    merged = run_tiles(packed, 0, live_total, gate_w, up_w, down_w)
    slot_out = jnp.where(
        live_row[:, None],
        merged[jnp.where(live_row, position, 0)],
        jnp.zeros((total_rows, width), jnp.bfloat16),
    )
    summed = lax.psum_scatter(
        slot_out.reshape(n_dp * n_exp, slot_cap, width), "dp", scatter_dimension=0, tiled=True
    ).astype(jnp.float32)
    expert_out = lax.all_to_all(
        summed.astype(jnp.bfloat16), "expert", split_axis=0, concat_axis=0, tiled=True
    )
    picked = expert_out.reshape(n_exp * slot_cap, width)[slot_idx]
    gate_wts = jnp.exp(gate_logits)
    gate_wts = gate_wts / jnp.sum(gate_wts, axis=1, keepdims=True)
    mixed = jnp.sum(
        picked.reshape(n_rows, n_tops, width).astype(jnp.float32) * gate_wts[:, :, None], axis=1
    )
    return mixed.astype(jnp.bfloat16)


def solution(mesh):
    return jax.shard_map(
        per_device,
        mesh=mesh,
        in_specs=(
            P(("expert", "dp"), None),
            P(("expert", "dp"), None),
            P(("expert", "dp"), None),
            P("expert", None, "dp"),
            P("expert", None, "dp"),
            P("expert", "dp", None),
        ),
        out_specs=P(("expert", "dp"), None),
        check_vma=False,
    )
```

profile of v0, /device:TPU:8, one launch (start us, length us, event | category | flops | bytes accessed | tf_op | source)
XLA Modules:
  0.0 599.4 jit_solution(584529033476823874)
XLA Ops:
  10.9 3.5 gather_fusion
  14.4 2.8 gather.17
  17.6 82.8 %all_to_all.22 = bf16[64,6,2880]{2,1,0:T(8,128)(2,1)S(1)} all-to-all(bf16[64,6,2880]{2,1,0:T(8,128)(2,1)S(1)} %broadcast_select_fusion.1), channel_id=1, replica_groups=mesh['expert'=64,'dp'=4] {'expert'}, dimensions={0} | all-to-all | bytes 4423680 | tf_op jit(solution)/shard_map/all_to_all | solution.py:51
  102.8 5.7 all-to-all-start
  108.6 3.0 copy.34
  112.9 4.2 all-to-all-done
  118.6 9.3 %all-reduce = s32[256]{0:T(256)S(1)} all-reduce(s32[256]{0:T(256)S(1)} %dynamic-update-slice), channel_id=2, replica_groups=mesh['expert'=64,'dp'=4] {'dp'}, use_global_device_ids=true, to_apply=%add | all-reduce | flops 256 | bytes 2048
  130.3 6.4 %scatter_custom_fusion.1 = s32[1664]{0:T(1024)S(1)} fusion(s32[1536]{0:T(1024)S(1)} %get-tuple-element.45, s32[1536]{0:T(1024)S(1)} %iota.22, s32[]{:T(128)} %constant.65.clone.1), kind=kCustom, calls=%fused_computation.57 | custom fusion | bytes 6660 | tf_op jit(solution)/shard_map/scatter | solution.py:67
  136.8 53.3 %all-gather.3.cloned.1.call-done = bf16[256,6,2880]{2,0,1:T(8,128)(2,1)} async-done(((bf16[64,6,2880]{2,0,1:T(8,128)(2,1)}), bf16[256,6,2880]{2,0,1:T(8,128)(2,1)}) %all-gather.3.cloned.1.call-update) | async-done | bytes 8847376 | tf_op jit(solution)/shard_map/all_gather | solution.py:55
  190.1 12.9 %copy.33 = bf16[256,6,2880]{2,1,0:T(8,128)(2,1)} copy(bf16[256,6,2880]{2,0,1:T(8,128)(2,1)} %all-gather.3.cloned.1.call-done) | data formatting | bytes 17694720 | tf_op jit(solution)/shard_map/all_gather | solution.py:55
  203.0 15.1 %reshape.195 = bf16[1536,2880]{1,0:T(8,128)(2,1)} reshape(bf16[256,6,2880]{2,1,0:T(8,128)(2,1)} %copy.33) | data formatting | bytes 17694720 | tf_op jit(solution)/shard_map/reshape | solution.py:58
  218.1 24.0 %gather_fusion.1 = bf16[1664,2880]{1,0:T(8,128)(2,1)} fusion(bf16[1536,2880]{1,0:T(8,128)(2,1)} %reshape.195, s32[2048]{0:T(1024)S(1)} %pad_clamp_fusion.1), kind=kCustom, calls=%fused_computation.1 | custom fusion | bytes 19175936 | tf_op jit(solution)/shard_map/gather | solution.py:69
  242.1 4.3 broadcast_in_dim.48
  246.4 45.9 %while.10 = (s32[]{:T(128)}, bf16[1664,2880]{0,1:T(8,128)(2,1)}, s32[]{:T(128)}, bf16[1664,2880]{1,0:T(8,128)(2,1)}, bf16[2880,384]{1,0:T(8,128)(2,1)}, /*index=...) while((s32[]{:T(128)}, bf16[1664,2880]{0,1:T(8,128)(2,1)}, ...), condition=%wide.region_10.11_spmd, body=%wide.region_9.10_spmd.sunk | while | flops 850108416 | bytes 9274527 | solution.py:26
  248.8 4.1 fusion.46
  255.4 4.2 fusion.46
  261.9 4.1 fusion.46
  268.5 4.2 fusion.46
  275.1 4.1 fusion.46
  281.6 4.1 fusion.46
  288.2 4.1 fusion.46
  292.3 14.0 %copy.35 = bf16[1664,2880]{1,0:T(8,128)(2,1)} copy(bf16[1664,2880]{0,1:T(8,128)(2,1)} %get-tuple-element.43) | data formatting | bytes 19169280 | tf_op jit(solution)/shard_map/while | solution.py:26
  306.3 21.9 %gather_fusion.2 = bf16[1536,2880]{1,0:T(8,128)(2,1)} fusion(bf16[1664,2880]{1,0:T(8,128)(2,1)} %copy.35, s32[2048]{0:T(1024)S(1)} %pad_clamp_fusion), kind=kCustom, calls=%fused_computation.2 | custom fusion | bytes 17700864 | tf_op jit(solution)/shard_map/gather | solution.py:76
  328.3 13.9 %gather.20 = bf16[256,6,2880]{2,1,0:T(8,128)(2,1)} reshape(bf16[1536,2880]{1,0:T(8,128)(2,1)} %gather_fusion.2) | data formatting | bytes 17694720 | tf_op jit(solution)/shard_map/gather | solution.py:76
  342.2 10.6 %broadcast_select_fusion = bf16[256,6,2880]{2,1,0:T(8,128)(2,1)} fusion(bf16[256,6,2880]{2,1,0:T(8,128)(2,1)} %gather.20, pred[256,6]{1,0:T(8,128)(4,1)S(1)} %get-tuple-element.63), kind=kLoop, calls=%fused_computation.26 | loop fusion | flops 4423680 | bytes 17696256 | tf_op jit(solution)/shard_map/jit(_where)/select_n | solution.py:74
  352.9 146.5 %reduce-scatter.2.cloned.1.call-done = bf16[64,6,2880]{2,1,0:T(8,128)(2,1)} async-done(((bf16[256,6,2880]{2,1,0:T(8,128)(2,1)}), bf16[64,6,2880]{2,1,0:T(8,128)(2,1)}) %reduce-scatter.2.cloned.1.call-update) | async-done | bytes 2211856 | tf_op jit(solution)/shard_map/reduce_scatter | solution.py:79
  499.4 10.7 %all-to-all-start.2 = ((bf16[64,6,2880]{2,1,0:T(8,128)(2,1)}), bf16[64,6,2880]{2,1,0:T(8,128)(2,1)}, u32[]{:S(2)}, u32[]{:S(2)}) async-start(bf16[64,6,2880]{2,1,0:T(8,128)(2,1)} %reduce-scatter.2.cloned.1.call-done), calls=%async_computation.3 | async-start | bytes 6029312 | tf_op jit(solution)/shard_map/all_to_all | solution.py:82
  510.3 70.7 %all-to-all-done.2 = bf16[64,6,2880]{2,1,0:T(8,128)(2,1)} async-done(((bf16[64,6,2880]{2,1,0:T(8,128)(2,1)}), bf16[64,6,2880]{2,1,0:T(8,128)(2,1)}, u32[]{:S(2)}, u32[]{:S(2)}) %all-to-all-start.2) | async-done | bytes 2211872 | tf_op jit(solution)/shard_map/all_to_all | solution.py:82
  580.9 3.3 reshape.197
  584.3 2.7 gather_fusion.3
  587.0 2.8 reshape.199
  589.8 2.8 multiply_reduce_fusion
  (62 shorter events, 28.1 us)
Async XLA Ops:
  6.5 4.4 copy-start
  6.5 183.6 %all-gather.3.cloned.1.call-start = ((), (), s32[]{:S(2)}) async-start(), calls=%async_computation.4 | async-start | bytes 11304960 | tf_op jit(solution)/shard_map/all_gather | solution.py:55
  102.1 9.6 %copy-start.3 = (u32[256]{0:T(256)S(1)}, u32[256]{0:T(256)}, u32[]{:S(2)}) copy-start(u32[256]{0:T(256)} %constant.87) | copy-start | bytes 3076
  102.8 14.3 %all-to-all-start = ((s32[64,1,1]{2,1,0:T(1,128)}), s32[64,1,1]{2,1,0:T(1,128)S(1)}, u32[]{:S(2)}, u32[]{:S(2)}) async-start(s32[64,1,1]{2,1,0:T(1,128)} %copy.28), calls=%async_computation | async-start | bytes 65536 | tf_op jit(solution)/shard_map/all_to_all | solution.py:52
  108.6 390.8 %reduce-scatter.2.cloned.1.call-start = ((), (), s32[]{:S(2)}) async-start(), calls=%async_computation.5 | async-start | bytes 15073280 | tf_op jit(solution)/shard_map/reduce_scatter | solution.py:79
  352.8 157.3 %copy-start.2 = (f32[64,4]{0,1:T(4,128)S(1)}, f32[64,4]{0,1:T(4,128)}, u32[]{:S(2)}) copy-start(f32[64,4]{0,1:T(4,128)} %param.10) | copy-start | bytes 3076
  499.4 81.6 %all-to-all-start.2 = ((bf16[64,6,2880]{2,1,0:T(8,128)(2,1)}), bf16[64,6,2880]{2,1,0:T(8,128)(2,1)}, u32[]{:S(2)}, u32[]{:S(2)}) async-start(bf16[64,6,2880]{2,1,0:T(8,128)(2,1)} %reduce-scatter.2.cloned.1.call-done), calls=%async_computation.3 | async-start | bytes 6029312 | tf_op jit(solution)/shard_map/all_to_all | solution.py:82
  584.3 8.3 %copy-start.1 = (bf16[64,2880]{1,0:T(8,128)(2,1)S(1)}, bf16[64,2880]{1,0:T(8,128)(2,1)}, u32[]{:S(2)}) copy-start(bf16[64,2880]{1,0:T(8,128)(2,1)} %param.8) | copy-start | bytes 1105924
Sparse Core Ops, SparseCore 0:
  102.3 87.7 all-gather.2
  353.0 146.3 reduce-scatter.1
where the time goes:
time: 602 us; the launch traced here: 599 us
  waiting for transfers between devices  275 us (46%)
  local copies, waits for them, and re-layouts  137 us (23%)
  blocking collectives  92.1 us (15%)
  matrix products  45.8 us (8%)
  other arithmetic  17.9 us (3%)
  starting transfers between devices  16.5 us (3%)
  between operations  15 us (2%)
    reduce_scatter x1, waiting for transfers between devices, per_device(): lax.psum_scatter(slot_out.reshape(n_dp * n_exp, slot_cap, width), 'dp', s...  147 us
    all_to_all x1, blocking collectives, per_device(): lax.all_to_all(outgoing, 'expert', split_axis=0, concat_axis=0, tiled=True)  82.8 us
    all_to_all x1, waiting for transfers between devices, per_device(): lax.all_to_all(summed.astype(jnp.bfloat16), 'expert', split_axis=0, conca...  70.7 us
    all_gather x1, waiting for transfers between devices, per_device(): lax.all_gather(rows_mid, 'dp', axis=0, tiled=True)  53.3 us
    gather x2, local copies, waits for them, and re-layouts, per_device(): merged[jnp.where(live_row, position, 0)]  35.8 us
    dot_general x7, matrix products, expert_rows(): jnp.dot(hidden, down_w, preferred_element_type=jnp.float32)  29 us
    gather x1, local copies, waits for them, and re-layouts, per_device(): packed = rows_flat[gather_idx]  24 us
    dot_general x7, matrix products, expert_rows(): gate_val = jnp.dot(tile_in, gate_w, preferred_element_type=jnp.float32)  16.9 us
  transfers between devices with their start and end apart: 4, of which 4 were waited for; matrix products, arithmetic and copies ran while one was open for 2% of the time, Pallas kernels for 0%

commit v1 on v0

--- a/solution.py
+++ b/solution.py
@@ -2,6 +2,12 @@
 import jax.numpy as jnp
 from jax import lax
 from jax.sharding import PartitionSpec as P
+
+
+def gather_from_all(x, axis, dim):
+    size = lax.axis_size(axis)
+    repeats = [size if d == dim else 1 for d in range(x.ndim)]
+    return lax.all_to_all(jnp.tile(x, repeats), axis, split_axis=dim, concat_axis=dim, tiled=True)
 
 
 def expert_rows(tile_in, gate_w, up_w, down_w):
@@ -52,7 +58,7 @@
         lax.all_to_all(counts[:, None], "expert", split_axis=0, concat_axis=0, tiled=True),
     )
     rows_in, counts_in = (
-        lax.all_gather(rows_mid, "dp", axis=0, tiled=True),
+        gather_from_all(rows_mid, "dp", 0),
         lax.all_gather(counts_mid, "dp", axis=0, tiled=True),
     )
     rows_flat = rows_in.reshape(-1, width)

time: 602 us -> 662 us (1.100)
  blocking collectives: 92.1 us -> 211 us
  waiting for transfers between devices: 275 us -> 211 us
  starting transfers between devices: 16.5 us -> 29.3 us
  local copies, waits for them, and re-layouts: 137 us -> 128 us
    unnamed x1, blocking collectives: 9.3 us -> 130 us
    all_gather x1 -> x0, waiting for transfers between devices: 53.3 us -> none  [per_device(): lax.all_gather(rows_mid, 'dp', axis=0, tiled=True)]
    all_gather x1 -> x0, local copies, waits for them, and re-layouts: 12.9 us -> none  [per_device(): lax.all_gather(rows_mid, 'dp', axis=0, tiled=True)]
  transfers between devices with their start and end apart: 4 -> 4, of which waited for: 4 -> 2; matrix products, arithmetic and copies ran while one was open for 2% -> 4% of each run, Pallas kernels for 0% -> 0%
where the time goes in v1:
time: 662 us; the launch traced here: 660 us
  waiting for transfers between devices  211 us (32%)
  blocking collectives  211 us (32%)
  local copies, waits for them, and re-layouts  128 us (19%)
  matrix products  45.8 us (7%)
  starting transfers between devices  29.3 us (4%)
  other arithmetic  19.5 us (3%)
  between operations  14.9 us (2%)
    reduce_scatter x1, waiting for transfers between devices, per_device(): lax.psum_scatter(slot_out.reshape(n_dp * n_exp, slot_cap, width), 'dp', s...  140 us
    unnamed x1, blocking collectives  130 us
    all_to_all x1, blocking collectives, per_device(): lax.all_to_all(outgoing, 'expert', split_axis=0, concat_axis=0, tiled=True)  81.2 us
    all_to_all x1, waiting for transfers between devices, per_device(): lax.all_to_all(summed.astype(jnp.bfloat16), 'expert', split_axis=0, conca...  70.7 us
    gather x2, local copies, waits for them, and re-layouts, per_device(): merged[jnp.where(live_row, position, 0)]  35.8 us
    dot_general x7, matrix products, expert_rows(): jnp.dot(hidden, down_w, preferred_element_type=jnp.float32)  29 us
    gather x1, local copies, waits for them, and re-layouts, per_device(): packed = rows_flat[gather_idx]  24 us
    dot_general x7, matrix products, expert_rows(): gate_val = jnp.dot(tile_in, gate_w, preferred_element_type=jnp.float32)  16.9 us
  transfers between devices with their start and end apart: 4, of which 2 were waited for; matrix products, arithmetic and copies ran while one was open for 4% of the time, Pallas kernels for 0%

profile of v1, /device:TPU:8, one launch (start us, length us, event | category | flops | bytes accessed | tf_op | source)
XLA Modules:
  0.0 659.6 jit_solution(6524451152656927642)
XLA Ops:
  9.3 12.1 %all-to-all-start = ((s32[64,1,1]{2,1,0:T(1,128)}), s32[64,1,1]{2,1,0:T(1,128)S(1)}, u32[]{:S(2)}, u32[]{:S(2)}) async-start(s32[64,1,1]{2,1,0:T(1,128)} %copy.26), calls=%async_computation | async-start | bytes 65536 | tf_op jit(solution)/shard_map/all_to_all | solution.py:58
  23.8 3.5 gather_fusion
  27.3 2.8 gather.17
  32.1 81.2 %all_to_all.27 = bf16[64,6,2880]{2,1,0:T(8,128)(2,1)S(1)} all-to-all(bf16[64,6,2880]{2,1,0:T(8,128)(2,1)} %broadcast_select_fusion.1), channel_id=1, replica_groups=mesh['expert'=64,'dp'=4] {'expert'}, dimensions={0} | all-to-all | bytes 4423680 | tf_op jit(solution)/shard_map/all_to_all | solution.py:57
  113.3 5.2 tile.4
  118.5 6.2 all-to-all-start.2
  124.8 2.9 copy.30
  130.4 129.9 %all-reduce = s32[256]{0:T(256)S(1)} all-reduce(s32[256]{0:T(256)S(1)} %dynamic-update-slice), channel_id=2, replica_groups=mesh['expert'=64,'dp'=4] {'dp'}, use_global_device_ids=true, to_apply=%add | all-reduce | flops 256 | bytes 2048
  262.7 6.4 scatter_custom_fusion.1
  269.1 15.1 %reshape.199 = bf16[1536,2880]{1,0:T(8,128)(2,1)} reshape(bf16[256,6,2880]{2,1,0:T(8,128)(2,1)} %all-to-all-done.2) | data formatting | bytes 17694720 | tf_op jit(solution)/shard_map/reshape | solution.py:64
  284.2 24.0 %gather_fusion.1 = bf16[1664,2880]{1,0:T(8,128)(2,1)} fusion(bf16[1536,2880]{1,0:T(8,128)(2,1)} %reshape.199, s32[2048]{0:T(1024)S(1)} %pad_clamp_fusion.1), kind=kCustom, calls=%fused_computation.1 | custom fusion | bytes 19175936 | tf_op jit(solution)/shard_map/gather | solution.py:75
  308.2 4.3 broadcast_in_dim.48
  312.5 45.9 %while.10 = (s32[]{:T(128)}, bf16[1664,2880]{0,1:T(8,128)(2,1)}, s32[]{:T(128)}, bf16[1664,2880]{1,0:T(8,128)(2,1)}, bf16[2880,384]{1,0:T(8,128)(2,1)}, /*index=...) while((s32[]{:T(128)}, bf16[1664,2880]{0,1:T(8,128)(2,1)}, ...), condition=%wide.region_10.11_spmd, body=%wide.region_9.10_spmd.sunk | while | flops 850108416 | bytes 9274527 | solution.py:32
  312.5 2.4 fusion.45
  314.9 4.1 fusion.46
  321.5 4.2 fusion.46
  328.1 4.1 fusion.46
  334.6 4.2 fusion.46
  341.2 4.1 fusion.46
  347.7 4.1 fusion.46
  354.3 4.1 fusion.46
  358.4 14.0 %copy.31 = bf16[1664,2880]{1,0:T(8,128)(2,1)} copy(bf16[1664,2880]{0,1:T(8,128)(2,1)} %get-tuple-element.43) | data formatting | bytes 19169280 | tf_op jit(solution)/shard_map/while | solution.py:32
  372.5 21.9 %gather_fusion.2 = bf16[1536,2880]{1,0:T(8,128)(2,1)} fusion(bf16[1664,2880]{1,0:T(8,128)(2,1)} %copy.31, s32[2048]{0:T(1024)S(1)} %pad_clamp_fusion), kind=kCustom, calls=%fused_computation.2 | custom fusion | bytes 17700864 | tf_op jit(solution)/shard_map/gather | solution.py:82
  394.4 13.9 %gather.20 = bf16[256,6,2880]{2,1,0:T(8,128)(2,1)} reshape(bf16[1536,2880]{1,0:T(8,128)(2,1)} %gather_fusion.2) | data formatting | bytes 17694720 | tf_op jit(solution)/shard_map/gather | solution.py:82
  408.3 10.6 %broadcast_select_fusion = bf16[256,6,2880]{2,1,0:T(8,128)(2,1)} fusion(bf16[256,6,2880]{2,1,0:T(8,128)(2,1)} %gather.20, pred[256,6]{1,0:T(8,128)(4,1)S(1)} %get-tuple-element.63), kind=kLoop, calls=%fused_computation.26 | loop fusion | flops 4423680 | bytes 17696256 | tf_op jit(solution)/shard_map/jit(_where)/select_n | solution.py:80
  419.0 140.4 %reduce-scatter.2.cloned.1.call-done = bf16[64,6,2880]{2,1,0:T(8,128)(2,1)} async-done(((bf16[256,6,2880]{2,1,0:T(8,128)(2,1)}), bf16[64,6,2880]{2,1,0:T(8,128)(2,1)}) %reduce-scatter.2.cloned.1.call-update) | async-done | bytes 2211856 | tf_op jit(solution)/shard_map/reduce_scatter | solution.py:85
  559.3 11.0 %all-to-all-start.3 = ((bf16[64,6,2880]{2,1,0:T(8,128)(2,1)}), bf16[64,6,2880]{2,1,0:T(8,128)(2,1)}, u32[]{:S(2)}, u32[]{:S(2)}) async-start(bf16[64,6,2880]{2,1,0:T(8,128)(2,1)} %reduce-scatter.2.cloned.1.call-done), calls=%async_computation.4 | async-start | bytes 6029312 | tf_op jit(solution)/shard_map/all_to_all | solution.py:88
  570.4 70.7 %all-to-all-done.3 = bf16[64,6,2880]{2,1,0:T(8,128)(2,1)} async-done(((bf16[64,6,2880]{2,1,0:T(8,128)(2,1)}), bf16[64,6,2880]{2,1,0:T(8,128)(2,1)}, u32[]{:S(2)}, u32[]{:S(2)}) %all-to-all-start.3) | async-done | bytes 2211872 | tf_op jit(solution)/shard_map/all_to_all | solution.py:88
  641.1 3.3 reshape.201
  644.5 2.7 gather_fusion.3
  647.2 2.8 reshape.203
  650.0 2.8 multiply_reduce_fusion
  (60 shorter events, 25.6 us)
Async XLA Ops:
  6.5 17.3 %copy-start = (bf16[64,2880]{1,0:T(8,128)(2,1)S(1)}, bf16[64,2880]{1,0:T(8,128)(2,1)}, u32[]{:S(2)}) copy-start(bf16[64,2880]{1,0:T(8,128)(2,1)} %param.8) | copy-start | bytes 1105924
  9.3 22.8 %all-to-all-start = ((s32[64,1,1]{2,1,0:T(1,128)}), s32[64,1,1]{2,1,0:T(1,128)S(1)}, u32[]{:S(2)}, u32[]{:S(2)}) async-start(s32[64,1,1]{2,1,0:T(1,128)} %copy.26), calls=%async_computation | async-start | bytes 65536 | tf_op jit(solution)/shard_map/all_to_all | solution.py:58
  118.5 150.6 %all-to-all-start.2 = ((bf16[256,6,2880]{2,1,0:T(8,128)(2,1)}), bf16[256,6,2880]{2,1,0:T(8,128)(2,1)}, u32[]{:S(2)}, u32[]{:S(2)}) async-start(bf16[256,6,2880]{2,1,0:T(8,128)(2,1)} %bitcast.42), calls=%async_computation.2 | async-start | bytes 24117248 | tf_op jit(solution)/shard_map/all_to_all | solution.py:10
  124.7 3.0 copy-start.3
  124.7 434.6 %reduce-scatter.2.cloned.1.call-start = ((), (), s32[]{:S(2)}) async-start(), calls=%async_computation.5 | async-start | bytes 15073280 | tf_op jit(solution)/shard_map/reduce_scatter | solution.py:85
  419.0 151.3 %copy-start.2 = (f32[64,4]{0,1:T(4,128)S(1)}, f32[64,4]{0,1:T(4,128)}, u32[]{:S(2)}) copy-start(f32[64,4]{0,1:T(4,128)} %param.10) | copy-start | bytes 3076
  559.3 81.8 %all-to-all-start.3 = ((bf16[64,6,2880]{2,1,0:T(8,128)(2,1)}), bf16[64,6,2880]{2,1,0:T(8,128)(2,1)}, u32[]{:S(2)}, u32[]{:S(2)}) async-start(bf16[64,6,2880]{2,1,0:T(8,128)(2,1)} %reduce-scatter.2.cloned.1.call-done), calls=%async_computation.4 | async-start | bytes 6029312 | tf_op jit(solution)/shard_map/all_to_all | solution.py:88
  644.5 8.3 %copy-start.1 = (bf16[64,2880]{1,0:T(8,128)(2,1)S(1)}, bf16[64,2880]{1,0:T(8,128)(2,1)}, u32[]{:S(2)}) copy-start(bf16[64,2880]{1,0:T(8,128)(2,1)} %param.8) | copy-start | bytes 1105924
Sparse Core Ops, SparseCore 0:
  419.1 140.2 reduce-scatter.1
